TPU v7x, 32 devices: a whole 2x2x4 slice. The times are simulated.
32 devices in a mesh: src: 8 (over z, core), tgt: 4 (over y, x).
Axes of the slice: x: 2, y: 2, z: 4, core: 2. Of those that a mesh axis runs over, the one named last changes fastest.
Arguments:
- source_embed: bfloat16 [128, 128, 128], P('src', None, 'tgt'), may hold values from -4 to 4
- target_embed: bfloat16 [64, 128, 128], P('tgt', None, 'src'), may hold values from -4 to 4
- source_mass: float32 [128, 128], P('src'), may hold values from 10 to 14
- target_mass: float32 [64, 128], P('tgt'), may hold values from 10 to 14
- target_start: float32 [64, 128], P('tgt'), may hold values from -6 to 6
- block_pairs: int32 [8, 4, 128, 2], P('src', 'tgt'), may hold values from 0 to 15, as said below
- counts: int32 [8, 4], P('src', 'tgt'), may hold values from 16 to 128, as said below
Outputs:
- sender_log_scaling: float32 [128, 128], P('src')
- target_dual_potential: float32 [64, 128], P('tgt')
Inputs may be any that keep to these rules, and one draw needn't show every extreme that they name: `block_pairs`: entry 0 of a slot is a local source block (below 16), entry 1 a local target block (below 16). The live slots of a device name distinct pairs; its first 16 slots name each of its target blocks once and each of its source blocks at least once. Slots at or past the device's count are not kept and hold arbitrary block numbers. `counts`: some device has all 128 slots live in every draw.
All inputs are finite; a program needn't handle non-finite values.
Results may differ from a plain program's by a relative error of at most 0.0003.
Values may be sent and summed in bfloat16 or wider, within the bound.
A program may use at most 64 MiB of HBM per device.

v0:
```python
import jax
import jax.numpy as jnp
from jax import lax
from jax.sharding import PartitionSpec as P

ITERS = 2
smoothing_epsilon = 4.0
empty_peak = -1e30
slot_batch = 8


def from_partner(block, axis, bit):
    count = lax.axis_size(axis)
    route = []
    for low in range(count):
        high = low | 1 << bit
        if high != low and high < count:
            route += [(low, high), (high, low)]
    return lax.ppermute(block, axis, route)


def absorb(maxima, totals, targets, block_peak, block_total):
    raised = maxima.at[targets].max(block_peak)
    totals = totals * jnp.exp(maxima - raised)
    totals = totals.at[targets].add(block_total * jnp.exp(block_peak - raised[targets]))
    return (raised, totals)


def combine_stats(first_pair, second_pair):
    joined = jnp.maximum(first_pair[0], second_pair[0])
    merged_sum = first_pair[1] * jnp.exp(first_pair[0] - joined) + second_pair[1] * jnp.exp(
        second_pair[0] - joined
    )
    return (joined, merged_sum)


def blank(blocks, frames):
    return (
        jnp.full((blocks, frames), empty_peak, jnp.float32),
        jnp.zeros((blocks, frames), jnp.float32),
    )


def block_stats(
    local_side, far_side, potential, slot_plan, column, first_slot, final_position_entry, running
):
    slot_count = slot_plan.shape[0]

    def group(counter, current):
        maxima, totals = current
        slot_ids = first_slot + counter * slot_batch + lax.iota(jnp.int32, slot_batch)
        usable = slot_ids < final_position_entry
        slot_ids = jnp.minimum(slot_ids, slot_count - 1)
        near = slot_plan[slot_ids, column]
        distant = slot_plan[slot_ids, 1 - column]
        similarity_matrix = (
            jnp.einsum(
                "fdg,fwg->fdw",
                local_side[near],
                far_side[distant],
                preferred_element_type=jnp.float32,
            )
            / smoothing_epsilon
        )
        similarity_matrix = similarity_matrix + potential[distant][:, None, :]
        block_peak = jnp.max(similarity_matrix, axis=2)
        block_total = jnp.sum(jnp.exp(similarity_matrix - block_peak[:, :, None]), axis=2)
        block_peak = jnp.where(usable[:, None], block_peak, empty_peak)
        block_total = jnp.where(usable[:, None], block_total, 0.0)
        return absorb(maxima, totals, near, block_peak, block_total)

    groups = jnp.maximum(final_position_entry - first_slot + slot_batch - 1, 0) // slot_batch
    return lax.fori_loop(0, groups, group, running)


def fold_rows(running):
    peak_all = lax.pmax(running[0], "tgt")
    summed = lax.psum(running[1] * jnp.exp(running[0] - peak_all), "tgt")
    result = (peak_all, summed)
    return result


def collapse_columns(running):
    peak_all = lax.pmax(running[0], "src")
    summed = lax.psum(running[1] * jnp.exp(running[0] - peak_all), "src")
    result = (peak_all, summed)
    return result


def finish(log_mass, running):
    return log_mass - (running[0] + jnp.log(running[1]))


def on_device(
    source_embed, target_embed, source_mass, target_mass, target_start, block_pairs, counts
):
    source_full = lax.all_gather(source_embed, "tgt", axis=2, tiled=True)
    target_full = lax.all_gather(target_embed, "src", axis=2, tiled=True)
    slot_plan = block_pairs.reshape(block_pairs.shape[2], 2)
    live_count = counts.reshape(())
    source_blocks = source_full.shape[0]
    target_blocks = target_full.shape[0]
    frames = source_full.shape[1]
    target_dual_potential = target_start
    sender_log_scaling = source_mass
    halfway = lax.axis_size("src").bit_length() - 2
    partner_full = from_partner(source_full, "src", halfway)
    partner_plan, matched_block_number = from_partner((slot_plan, live_count), "src", halfway)
    shared = (live_count + matched_block_number + 1) // 2
    own_last = jnp.minimum(live_count, shared)
    lent_first = jnp.minimum(matched_block_number, shared)
    for iteration in range(ITERS):
        running = block_stats(
            source_full,
            target_full,
            target_dual_potential,
            slot_plan,
            0,
            0,
            own_last,
            blank(source_blocks, frames),
        )
        lent = block_stats(
            partner_full,
            target_full,
            target_dual_potential,
            partner_plan,
            0,
            lent_first,
            matched_block_number,
            blank(source_blocks, frames),
        )
        returned = from_partner((lent[0], lent[1]), "src", halfway)
        running = combine_stats(running, returned)
        sender_log_scaling = finish(source_mass, fold_rows(running))
        partner_pot = from_partner(sender_log_scaling, "src", halfway)
        running = block_stats(
            target_full,
            source_full,
            sender_log_scaling,
            slot_plan,
            1,
            0,
            own_last,
            blank(target_blocks, frames),
        )
        running = block_stats(
            target_full,
            partner_full,
            partner_pot,
            partner_plan,
            1,
            lent_first,
            matched_block_number,
            running,
        )
        target_dual_potential = finish(target_mass, collapse_columns(running))
    return (sender_log_scaling, target_dual_potential)


def solution(mesh):
    in_specs = (
        P("src", None, "tgt"),
        P("tgt", None, "src"),
        P("src", None),
        P("tgt", None),
        P("tgt", None),
        P("src", "tgt", None, None),
        P("src", "tgt"),
    )
    out_specs = (P("src", None), P("tgt", None))
    return jax.shard_map(
        on_device, mesh=mesh, in_specs=in_specs, out_specs=out_specs, check_vma=False
    )
```

profile of v0, /device:TPU:3, one launch (start us, length us, event | category | flops | bytes accessed | tf_op | source)
XLA Modules:
  0.0 464.4 jit_solution(17082557890183272998)
XLA Ops:
  0.6 1.0 copy.13
  1.6 8.0 %all_gather.6 = bf16[16,128,128]{1,0,2:T(8,128)(2,1)S(1)} all-gather(bf16[16,128,32]{1,0,2:T(8,128)(2,1)S(1)} %copy.13), channel_id=1, replica_groups=mesh['src'=8,'tgt'=4] {'tgt'}, dimensions={2}, use_global_device_ids=true | all-gather | bytes 655360 | tf_op jit(solution)/shard_map/all_gather | solution.py:97
  9.6 2.3 collective-permute-start.2
  12.6 1.7 collective-permute-start.1
  15.8 30.6 %all_gather.7 = bf16[16,128,128]{1,0,2:T(8,128)(2,1)S(1)} all-gather(bf16[16,128,16]{1,0,2:T(8,128)(2,1)S(1)} %copy.14), channel_id=1, replica_groups=mesh['src'=8,'tgt'=4] {'src'}, dimensions={2}, use_global_device_ids=true | all-gather | bytes 589824 | tf_op jit(solution)/shard_map/all_gather | solution.py:98
  49.5 0.7 copy-done.1
  50.5 2.0 collective-permute-start.4
  52.5 10.0 %while.96 = (s32[]{:T(128)}, f32[16,128]{1,0:T(8,128)S(1)}, f32[16,128]{1,0:T(8,128)S(1)}, s32[]{:T(128)}, s32[128,2]{0,1:T(2,128)S(1)}, /*index=5*/s32[]{:T(128...) while((s32[]{:T(128)}, f32[16,128]{1,0:T(8,128)S(1)}, ...), condition=%wide.region_5.6_spmd, body=%wide.region_0.5_spmd.sunk | while | flops 34221184 | bytes 2762505 | solution.py:73
  52.6 0.7 gather_fusion
  53.8 0.7 gather_fusion.1
  56.1 0.7 scatter_custom_fusion.66
  56.8 0.7 scatter_custom_fusion.67
  57.6 0.7 gather_fusion
  58.9 0.7 gather_fusion.1
  61.1 0.7 scatter_custom_fusion.66
  61.9 0.7 scatter_custom_fusion.67
  62.6 35.8 %pmax.28 = f32[16,128]{1,0:T(8,128)S(1)} all-reduce(f32[16,128]{1,0:T(8,128)S(1)} %max.44), channel_id=1, replica_groups=mesh['src'=8,'tgt'=4] {'tgt'}, use_global_device_ids=true, to_apply=%region_12.13 | all-reduce | flops 2048 | bytes 16384 | tf_op jit(solution)/shard_map/pmax | solution.py:77
  98.5 5.9 %psum.28 = f32[16,128]{1,0:T(8,128)S(1)} all-reduce(f32[16,128]{1,0:T(8,128)S(1)} %exponential_multiply_fusion.11), channel_id=1, replica_groups=mesh['src'=8,'tgt'=4] {'tgt'}, use_global_device_ids=true, to_apply=%region_13.14 | all-reduce | flops 2048 | bytes 16384 | tf_op jit(solution)/shard_map/psum | solution.py:78
  105.0 8.7 %collective-permute-start.5 = (f32[16,128]{1,0:T(8,128)}, f32[16,128]{1,0:T(8,128)S(1)}, u32[]{:S(2)}, u32[]{:S(2)}) collective-permute-start(f32[16,128]{1,0:T(8,128)} %add_subtract_fusion.3), channel_id=1, source_target_pairs={{0,16},{16,0},{4,20},{20,4},{8,24},{24,8},{12,28},{28,12},{1,17},{... | collective-permute-start | bytes 24584 | tf_op jit(solution)/shard_map/ppermute | solution.py:19
  113.7 11.4 %while.98 = (s32[]{:T(128)}, f32[16,128]{1,0:T(8,128)S(1)}, f32[16,128]{1,0:T(8,128)S(1)}, s32[]{:T(128)}, s32[128,2]{0,1:T(2,128)S(1)}, /*index=5*/s32[]{:T(128...) while((s32[]{:T(128)}, f32[16,128]{1,0:T(8,128)S(1)}, ...), condition=%wide.region_19.20_spmd, body=%wide.region_14.19_spmd.sunk | while | flops 34221184 | bytes 2762505 | solution.py:73
  115.0 0.7 gather_fusion.11
  116.3 1.3 gather_fusion.12
  118.0 0.7 scatter_custom_fusion.74
  118.7 0.7 scatter_custom_fusion.75
  122.0 1.3 gather_fusion.12
  123.7 0.7 scatter_custom_fusion.74
  124.4 0.7 scatter_custom_fusion.75
  125.2 117.4 %pmax.29 = f32[16,128]{1,0:T(8,128)S(1)} all-reduce(f32[16,128]{1,0:T(8,128)S(1)} %get-tuple-element.420), channel_id=1, replica_groups=mesh['src'=8,'tgt'=4] {'src'}, use_global_device_ids=true, to_apply=%region_26.27 | all-reduce | flops 2048 | bytes 16384 | tf_op jit(solution)/shard_map/pmax | solution.py:84
  242.7 14.0 %psum.29 = f32[16,128]{1,0:T(8,128)S(1)} all-reduce(f32[16,128]{1,0:T(8,128)S(1)} %exponential_multiply_fusion.10), channel_id=1, replica_groups=mesh['src'=8,'tgt'=4] {'src'}, use_global_device_ids=true, to_apply=%region_27.28 | all-reduce | flops 2048 | bytes 16384 | tf_op jit(solution)/shard_map/psum | solution.py:85
  256.9 2.4 collective-permute-start.7
  259.2 10.0 %while.100 = (s32[]{:T(128)}, f32[16,128]{1,0:T(8,128)S(1)}, f32[16,128]{1,0:T(8,128)S(1)}, s32[]{:T(128)}, s32[128,2]{0,1:T(2,128)S(1)}, /*index=5*/s32[]{:T(12...) while((s32[]{:T(128)}, f32[16,128]{1,0:T(8,128)S(1)}, ...), condition=%wide.region_33.34_spmd, body=%wide.region_28.33_spmd.sunk | while | flops 34221184 | bytes 2762505 | solution.py:73
  259.2 0.7 gather_fusion.20
  260.5 0.7 gather_fusion.21
  262.8 0.7 scatter_custom_fusion.82
  263.5 0.7 scatter_custom_fusion.83
  267.8 0.7 scatter_custom_fusion.82
  268.5 0.7 scatter_custom_fusion.83
  269.3 25.2 %pmax.30 = f32[16,128]{1,0:T(8,128)S(1)} all-reduce(f32[16,128]{1,0:T(8,128)S(1)} %max.45), channel_id=1, replica_groups=mesh['src'=8,'tgt'=4] {'tgt'}, use_global_device_ids=true, to_apply=%region_40.41 | all-reduce | flops 2048 | bytes 16384 | tf_op jit(solution)/shard_map/pmax | solution.py:77
  294.5 5.9 %psum.30 = f32[16,128]{1,0:T(8,128)S(1)} all-reduce(f32[16,128]{1,0:T(8,128)S(1)} %exponential_multiply_fusion.9), channel_id=1, replica_groups=mesh['src'=8,'tgt'=4] {'tgt'}, use_global_device_ids=true, to_apply=%region_41.42 | all-reduce | flops 2048 | bytes 16384 | tf_op jit(solution)/shard_map/psum | solution.py:78
  301.0 11.4 %while.102 = (s32[]{:T(128)}, f32[16,128]{1,0:T(8,128)S(1)}, f32[16,128]{1,0:T(8,128)S(1)}, s32[]{:T(128)}, s32[128,2]{0,1:T(2,128)S(1)}, /*index=5*/s32[]{:T(12...) while((s32[]{:T(128)}, f32[16,128]{1,0:T(8,128)S(1)}, ...), condition=%wide.region_47.48_spmd, body=%wide.region_42.47_spmd.sunk | while | flops 34221184 | bytes 2762505 | solution.py:73
  303.6 1.3 gather_fusion.32
  305.3 0.7 scatter_custom_fusion.90
  306.0 0.7 scatter_custom_fusion.91
  309.3 1.3 gather_fusion.32
  311.0 0.7 scatter_custom_fusion.90
  311.7 0.7 scatter_custom_fusion.91
  312.5 137.2 %pmax.31 = f32[16,128]{1,0:T(8,128)S(1)} all-reduce(f32[16,128]{1,0:T(8,128)S(1)} %get-tuple-element.428), channel_id=1, replica_groups=mesh['src'=8,'tgt'=4] {'src'}, use_global_device_ids=true, to_apply=%region_54.55 | all-reduce | flops 2048 | bytes 16384 | tf_op jit(solution)/shard_map/pmax | solution.py:84
  449.7 14.0 %psum.31 = f32[16,128]{1,0:T(8,128)S(1)} all-reduce(f32[16,128]{1,0:T(8,128)S(1)} %exponential_multiply_fusion.8), channel_id=1, replica_groups=mesh['src'=8,'tgt'=4] {'src'}, use_global_device_ids=true, to_apply=%region_55.56 | all-reduce | flops 2048 | bytes 16384 | tf_op jit(solution)/shard_map/psum | solution.py:85
  (169 shorter events, 26.3 us)
Async XLA Ops:
  9.6 39.4 %collective-permute-start.2 = (bf16[16,128,128]{1,0,2:T(8,128)(2,1)S(1)}, bf16[16,128,128]{1,0,2:T(8,128)(2,1)S(1)}, u32[]{:S(2)}, u32[]{:S(2)}) collective-permute-start(bf16[16,128,128]{1,0,2:T(8,128)(2,1)S(1)} %all_gather.6), channel_id=1, source_target_pairs={{0,16},{16,0},{4,20},{20,4},{8,24},{24,8},{12,28},{28,12},{1,17},{... | collective-permute-start | bytes 1572872 | tf_op jit(solution)/shard_map/ppermute | solution.py:19
  11.9 0.7 copy-start
  11.9 34.9 %collective-permute-start = (s32[]{:T(128)}, s32[]{:T(128)}, u32[]{:S(2)}, u32[]{:S(2)}) collective-permute-start(s32[]{:T(128)} %bitcast.48), channel_id=1, source_target_pairs={{0,16},{16,0},{4,20},{20,4},{8,24},{24,8},{12,28},{28,12},{1,17},{... | collective-permute-start | bytes 20 | tf_op jit(solution)/shard_map/ppermute | solution.py:19
  12.6 36.9 %collective-permute-start.1 = (s32[128,2]{0,1:T(2,128)S(1)}, s32[128,2]{0,1:T(2,128)S(1)}, u32[]{:S(2)}, u32[]{:S(2)}) collective-permute-start(s32[128,2]{0,1:T(2,128)S(1)} %bitcast.228), channel_id=1, source_target_pairs={{0,16},{16,0},{4,20},{20,4},{8,24},{24,8},{12,28},{28,12},{1,17},{... | collective-permute-start | bytes 3080 | tf_op jit(solution)/shard_map/ppermute | solution.py:19
  14.9 0.8 copy-start.2
  49.5 0.7 copy-start.1
  50.2 12.4 %collective-permute-start.3 = (f32[16,128]{1,0:T(8,128)S(1)}, f32[16,128]{1,0:T(8,128)S(1)}, u32[]{:S(2)}, u32[]{:S(2)}) collective-permute-start(f32[16,128]{1,0:T(8,128)S(1)} %get-tuple-element.415), channel_id=1, source_target_pairs={{0,16},{16,0},{4,20},{20,4},{8,24},{24,8},{12,28},{28,12},{1,17},{... | collective-permute-start | bytes 24584 | tf_op jit(solution)/shard_map/ppermute | solution.py:19
  50.5 47.9 %collective-permute-start.4 = (f32[16,128]{1,0:T(8,128)S(1)}, f32[16,128]{1,0:T(8,128)S(1)}, u32[]{:S(2)}, u32[]{:S(2)}) collective-permute-start(f32[16,128]{1,0:T(8,128)S(1)} %get-tuple-element.417), channel_id=1, source_target_pairs={{0,16},{16,0},{4,20},{20,4},{8,24},{24,8},{12,28},{28,12},{1,17},{... | collective-permute-start | bytes 24584 | tf_op jit(solution)/shard_map/ppermute | solution.py:19
  98.5 5.9 %copy-start.3 = (f32[16,128]{1,0:T(8,128)S(1)}, f32[16,128]{1,0:T(8,128)}, u32[]{:S(2)}) copy-start(f32[16,128]{1,0:T(8,128)} %param.25) | copy-start | bytes 24580
  105.0 20.2 %collective-permute-start.5 = (f32[16,128]{1,0:T(8,128)}, f32[16,128]{1,0:T(8,128)S(1)}, u32[]{:S(2)}, u32[]{:S(2)}) collective-permute-start(f32[16,128]{1,0:T(8,128)} %add_subtract_fusion.3), channel_id=1, source_target_pairs={{0,16},{16,0},{4,20},{20,4},{8,24},{24,8},{12,28},{28,12},{1,17},{... | collective-permute-start | bytes 24584 | tf_op jit(solution)/shard_map/ppermute | solution.py:19
  242.7 14.1 %copy-start.4 = (f32[16,128]{1,0:T(8,128)S(1)}, f32[16,128]{1,0:T(8,128)}, u32[]{:S(2)}) copy-start(f32[16,128]{1,0:T(8,128)} %param.26) | copy-start | bytes 24580
  256.8 12.5 %collective-permute-start.6 = (f32[16,128]{1,0:T(8,128)S(1)}, f32[16,128]{1,0:T(8,128)S(1)}, u32[]{:S(2)}, u32[]{:S(2)}) collective-permute-start(f32[16,128]{1,0:T(8,128)S(1)} %get-tuple-element.423), channel_id=1, source_target_pairs={{0,16},{16,0},{4,20},{20,4},{8,24},{24,8},{12,28},{28,12},{1,17},{... | collective-permute-start | bytes 24584 | tf_op jit(solution)/shard_map/ppermute | solution.py:19
  256.9 37.6 %collective-permute-start.7 = (f32[16,128]{1,0:T(8,128)S(1)}, f32[16,128]{1,0:T(8,128)S(1)}, u32[]{:S(2)}, u32[]{:S(2)}) collective-permute-start(f32[16,128]{1,0:T(8,128)S(1)} %get-tuple-element.425), channel_id=1, source_target_pairs={{0,16},{16,0},{4,20},{20,4},{8,24},{24,8},{12,28},{28,12},{1,17},{... | collective-permute-start | bytes 24584 | tf_op jit(solution)/shard_map/ppermute | solution.py:19
  301.0 11.4 %collective-permute-start.8 = (f32[16,128]{1,0:T(8,128)}, f32[16,128]{1,0:T(8,128)S(1)}, u32[]{:S(2)}, u32[]{:S(2)}) collective-permute-start(f32[16,128]{1,0:T(8,128)} %add_subtract_fusion.1), channel_id=1, source_target_pairs={{0,16},{16,0},{4,20},{20,4},{8,24},{24,8},{12,28},{28,12},{1,17},{... | collective-permute-start | bytes 24584 | tf_op jit(solution)/shard_map/ppermute | solution.py:19
where the time goes:
time: 467 us; the launch traced here: 464 us
  blocking collectives  394 us (84%)
  local copies, waits for them, and re-layouts  31.4 us (7%)
  starting transfers between devices  17.6 us (4%)
  other arithmetic  14.1 us (3%)
    pmax x2, blocking collectives, collapse_columns(): peak_all = lax.pmax(running[0], 'src')  255 us
    pmax x2, blocking collectives, fold_rows(): peak_all = lax.pmax(running[0], 'tgt')  61 us
    all_gather x1, blocking collectives, on_device(): target_full = lax.all_gather(target_embed, 'src', axis=2, tiled=True)  30.6 us
    psum x2, blocking collectives, collapse_columns(): summed = lax.psum(running[1] * jnp.exp(running[0] - peak_all), 'src')  28.1 us
    ppermute x9, starting transfers between devices, from_partner(): return lax.ppermute(block, axis, route)  17.6 us
    psum x2, blocking collectives, fold_rows(): summed = lax.psum(running[1] * jnp.exp(running[0] - peak_all), 'tgt')  11.8 us
  transfers between devices with their start and end apart: 9, of which 0 were waited for; matrix products, arithmetic and copies ran while one was open for 9% of the time, Pallas kernels for 0%

commit v1 on v0

--- a/solution.py
+++ b/solution.py
@@ -95,7 +95,31 @@
     source_embed, target_embed, source_mass, target_mass, target_start, block_pairs, counts
 ):
     source_full = lax.all_gather(source_embed, "tgt", axis=2, tiled=True)
-    target_full = lax.all_gather(target_embed, "src", axis=2, tiled=True)
+    local_out = lax.psum(1, "src")
+    seen_now, back, val = (local_out, lax.axis_index("src"), target_embed.shape[2])
+    shelf = []
+    for k, at in enumerate(target_embed.shape):
+        shelf.append(at * seen_now if k == 2 else at)
+    target_full = lax.dynamic_update_slice_in_dim(
+        jnp.zeros(shelf, target_embed.dtype), target_embed, back * val, axis=2
+    )
+    shaped = far_arr = target_embed
+    for u in tuple(range(1, seen_now // 2 + 1)):
+        trail = []
+        for k in tuple(range(seen_now)):
+            trail.append((k, (k + 1) % seen_now))
+        shaped = lax.ppermute(shaped, "src", trail)
+        target_full = lax.dynamic_update_slice_in_dim(
+            target_full, shaped, (back - u) % seen_now * val, axis=2
+        )
+        if 2 * u < seen_now:
+            inbox = []
+            for k in [*range(seen_now)]:
+                inbox.append((k, (k - 1) % seen_now))
+            far_arr = lax.ppermute(far_arr, "src", inbox)
+            target_full = lax.dynamic_update_slice_in_dim(
+                target_full, far_arr, (back + u) % seen_now * val, axis=2
+            )
     slot_plan = block_pairs.reshape(block_pairs.shape[2], 2)
     live_count = counts.reshape(())
     source_blocks = source_full.shape[0]

time: 467 us -> 539 us (1.15)
  local copies, waits for them, and re-layouts: 31.4 us -> 74.2 us
  waiting for transfers between devices: 0.02 us -> 31.2 us
  blocking collectives: 394 us -> 370 us
  starting transfers between devices: 17.6 us -> 40.5 us
    dynamic_update_slice x0 -> x8, local copies, waits for them, and re-layouts: none -> 43.9 us  [the longest x4 20.4 us: on_device(): lax.dynamic_update_slice_in_dim(target_full, shaped, (back - u) % seen_no...]
    ppermute x0 -> x7, waiting for transfers between devices: none -> 31.2 us  [the longest x4 21.1 us: on_device(): shaped = lax.ppermute(shaped, 'src', trail)]
    all_gather x1 -> x0, blocking collectives: 30.6 us -> none  [on_device(): target_full = lax.all_gather(target_embed, 'src', axis=2, tiled=True)]
    ppermute x0 -> x7, starting transfers between devices: none -> 24.3 us  [the longest x4 23.2 us: on_device(): shaped = lax.ppermute(shaped, 'src', trail)]
  transfers between devices with their start and end apart: 9 -> 16, of which waited for: 0 -> 3; matrix products, arithmetic and copies ran while one was open for 9% -> 16% of each run, Pallas kernels for 0% -> 0%
where the time goes in v1:
time: 539 us; the launch traced here: 537 us
  blocking collectives  370 us (69%)
  local copies, waits for them, and re-layouts  74.2 us (14%)
  starting transfers between devices  40.5 us (8%)
  waiting for transfers between devices  31.2 us (6%)
  other arithmetic  14.1 us (3%)
    pmax x2, blocking collectives, collapse_columns(): peak_all = lax.pmax(running[0], 'src')  257 us
    pmax x2, blocking collectives, fold_rows(): peak_all = lax.pmax(running[0], 'tgt')  64.8 us
    psum x2, blocking collectives, collapse_columns(): summed = lax.psum(running[1] * jnp.exp(running[0] - peak_all), 'src')  28.1 us
    ppermute x4, starting transfers between devices, on_device(): shaped = lax.ppermute(shaped, 'src', trail)  23.2 us
    ppermute x4, waiting for transfers between devices, on_device(): shaped = lax.ppermute(shaped, 'src', trail)  21.1 us
    dynamic_update_slice x4, local copies, waits for them, and re-layouts, on_device(): lax.dynamic_update_slice_in_dim(target_full, shaped, (back - u) % seen_no...  20.4 us
    dynamic_update_slice x3, local copies, waits for them, and re-layouts, on_device(): lax.dynamic_update_slice_in_dim(target_full, far_arr, (back + u) % seen_n...  18.4 us
    ppermute x9, starting transfers between devices, from_partner(): return lax.ppermute(block, axis, route)  16.2 us
  transfers between devices with their start and end apart: 16, of which 3 were waited for; matrix products, arithmetic and copies ran while one was open for 16% of the time, Pallas kernels for 0%

profile of v1, /device:TPU:3, one launch (start us, length us, event | category | flops | bytes accessed | tf_op | source)
XLA Modules:
  0.0 536.7 jit_solution(4563557694879774276)
XLA Ops:
  0.6 1.0 copy.17
  1.6 8.2 %all_gather.3 = bf16[16,128,128]{1,0,2:T(8,128)(2,1)S(1)} all-gather(bf16[16,128,32]{1,0,2:T(8,128)(2,1)S(1)} %copy.17), channel_id=1, replica_groups=mesh['src'=8,'tgt'=4] {'tgt'}, dimensions={2}, use_global_device_ids=true | all-gather | bytes 655360 | tf_op jit(solution)/shard_map/all_gather | solution.py:97
  9.8 2.3 collective-permute-start.9
  12.4 4.2 collective-permute-start.1
  16.6 15.4 %collective-permute-done.1 = bf16[16,128,16]{2,1,0:T(8,128)(2,1)S(1)} collective-permute-done((bf16[16,128,16]{2,1,0:T(8,128)(2,1)S(1)}, bf16[16,128,16]{2,1,0:T(8,128)(2,1)S(1)}, u32[]{:S(2)}, u32[]{:S(2)}) %collective-permute-start.1) | collective-permute-done | bytes 65568 | tf_op jit(solution)/shard_map/ppermute | solution.py:111
  32.0 2.5 collective-permute-start.3
  34.5 1.2 collective-permute-start.4
  35.6 5.7 %collective-permute-done.3 = bf16[16,128,16]{2,1,0:T(8,128)(2,1)S(1)} collective-permute-done((bf16[16,128,16]{2,1,0:T(8,128)(2,1)S(1)}, bf16[16,128,16]{2,1,0:T(8,128)(2,1)S(1)}, u32[]{:S(2)}, u32[]{:S(2)}) %collective-permute-start.3) | collective-permute-done | bytes 65568 | tf_op jit(solution)/shard_map/ppermute | solution.py:111
  41.3 13.7 %collective-permute-start.5 = (bf16[16,128,16]{2,1,0:T(8,128)(2,1)S(1)}, bf16[16,128,16]{2,1,0:T(8,128)(2,1)}, u32[]{:S(2)}, u32[]{:S(2)}) collective-permute-start(bf16[16,128,16]{2,1,0:T(8,128)(2,1)S(1)} %collective-permute-done.3), channel_id=1, source_target_pairs={{0,4},{4,8},{8,12},{12,16},{16,20},{20,24},{24,28},{28,0},{1,5},{5... | collective-permute-start | bytes 196616 | tf_op jit(solution)/shard_map/ppermute | solution.py:111
  55.1 10.0 %collective-permute-done.4 = bf16[16,128,16]{2,1,0:T(8,128)(2,1)} collective-permute-done((bf16[16,128,16]{2,1,0:T(8,128)(2,1)S(1)}, bf16[16,128,16]{2,1,0:T(8,128)(2,1)}, u32[]{:S(2)}, u32[]{:S(2)}) %collective-permute-start.4) | collective-permute-done | bytes 65568 | tf_op jit(solution)/shard_map/ppermute | solution.py:119
  65.1 2.8 collective-permute-start.7
  67.9 1.8 collective-permute-start
  71.6 5.1 dynamic_update_slice.24
  78.4 1.9 dynamic_update_slice.25
  80.4 5.1 dynamic_update_slice.26
  85.5 5.1 dynamic_update_slice.27
  90.6 6.7 %dynamic_update_slice.28 = bf16[16,128,128]{2,1,0:T(8,128)(2,1)S(1)} dynamic-update-slice(bf16[16,128,128]{2,1,0:T(8,128)(2,1)S(1)} %dynamic_update_slice.27, bf16[16,128,16]{2,1,0:T(8,128)(2,1)} %collective-permute-done.4, s32[]{:T(128)} %copy.143, s32[]{:T(128)} %copy.143, s32[]{:T(128)S(6)} %select_n.410) | dynamic-update-slice | bytes 131076 | tf_op jit(solution)/shard_map/dynamic_update_slice | solution.py:120
  97.2 6.7 %dynamic_update_slice.29 = bf16[16,128,128]{2,1,0:T(8,128)(2,1)S(1)} dynamic-update-slice(bf16[16,128,128]{2,1,0:T(8,128)(2,1)S(1)} %dynamic_update_slice.28, bf16[16,128,16]{2,1,0:T(8,128)(2,1)} %collective-permute-done.5, s32[]{:T(128)} %copy.143, s32[]{:T(128)} %copy.143, s32[]{:T(128)S(6)} %select_n.412) | dynamic-update-slice | bytes 131076 | tf_op jit(solution)/shard_map/dynamic_update_slice | solution.py:112
  103.9 6.7 %dynamic_update_slice.30 = bf16[16,128,128]{2,1,0:T(8,128)(2,1)S(1)} dynamic-update-slice(bf16[16,128,128]{2,1,0:T(8,128)(2,1)S(1)} %dynamic_update_slice.29, bf16[16,128,16]{2,1,0:T(8,128)(2,1)} %collective-permute-done.6, s32[]{:T(128)} %copy.143, s32[]{:T(128)} %copy.143, s32[]{:T(128)S(6)} %select_n.414) | dynamic-update-slice | bytes 131076 | tf_op jit(solution)/shard_map/dynamic_update_slice | solution.py:120
  110.6 6.7 %dynamic_update_slice.31 = bf16[16,128,128]{2,1,0:T(8,128)(2,1)S(1)} dynamic-update-slice(bf16[16,128,128]{2,1,0:T(8,128)(2,1)S(1)} %dynamic_update_slice.30, bf16[16,128,16]{2,1,0:T(8,128)(2,1)} %collective-permute-done.7, s32[]{:T(128)} %copy.143, s32[]{:T(128)} %copy.143, s32[]{:T(128)S(6)} %select_n.416) | dynamic-update-slice | bytes 131076 | tf_op jit(solution)/shard_map/dynamic_update_slice | solution.py:112
  118.5 2.9 collective-permute-start.10
  121.5 10.0 %while.96 = (s32[]{:T(128)}, f32[16,128]{1,0:T(8,128)S(1)}, f32[16,128]{1,0:T(8,128)S(1)}, s32[]{:T(128)}, s32[128,2]{0,1:T(2,128)S(1)}, /*index=5*/s32[]{:T(128...) while((s32[]{:T(128)}, f32[16,128]{1,0:T(8,128)S(1)}, ...), condition=%wide.region_5.6_spmd, body=%wide.region_0.5_spmd.sunk | while | flops 34221184 | bytes 2762505 | solution.py:73
  125.0 0.7 scatter_custom_fusion.66
  125.7 0.7 scatter_custom_fusion.67
  130.8 0.7 scatter_custom_fusion.67
  131.5 37.5 %pmax.28 = f32[16,128]{1,0:T(8,128)S(1)} all-reduce(f32[16,128]{1,0:T(8,128)S(1)} %max.44), channel_id=1, replica_groups=mesh['src'=8,'tgt'=4] {'tgt'}, use_global_device_ids=true, to_apply=%region_12.13 | all-reduce | flops 2048 | bytes 16384 | tf_op jit(solution)/shard_map/pmax | solution.py:77
  169.1 5.9 %psum.28 = f32[16,128]{1,0:T(8,128)S(1)} all-reduce(f32[16,128]{1,0:T(8,128)S(1)} %exponential_multiply_fusion.11), channel_id=1, replica_groups=mesh['src'=8,'tgt'=4] {'tgt'}, use_global_device_ids=true, to_apply=%region_13.14 | all-reduce | flops 2048 | bytes 16384 | tf_op jit(solution)/shard_map/psum | solution.py:78
  175.6 6.1 %collective-permute-start.12 = (f32[16,128]{1,0:T(8,128)}, f32[16,128]{1,0:T(8,128)S(1)}, u32[]{:S(2)}, u32[]{:S(2)}) collective-permute-start(f32[16,128]{1,0:T(8,128)} %add_subtract_fusion.3), channel_id=1, source_target_pairs={{0,16},{16,0},{4,20},{20,4},{8,24},{24,8},{12,28},{28,12},{1,17},{... | collective-permute-start | bytes 24584 | tf_op jit(solution)/shard_map/ppermute | solution.py:19
  181.6 11.4 %while.98 = (s32[]{:T(128)}, f32[16,128]{1,0:T(8,128)S(1)}, f32[16,128]{1,0:T(8,128)S(1)}, s32[]{:T(128)}, s32[128,2]{0,1:T(2,128)S(1)}, /*index=5*/s32[]{:T(128...) while((s32[]{:T(128)}, f32[16,128]{1,0:T(8,128)S(1)}, ...), condition=%wide.region_19.20_spmd, body=%wide.region_14.19_spmd.sunk | while | flops 34221184 | bytes 2762505 | solution.py:73
  184.2 1.3 gather_fusion.12
  186.6 0.7 scatter_custom_fusion.75
  189.9 1.3 gather_fusion.12
  192.3 0.7 scatter_custom_fusion.75
  193.3 123.4 %pmax.29 = f32[16,128]{1,0:T(8,128)S(1)} all-reduce(f32[16,128]{1,0:T(8,128)S(1)} %get-tuple-element.420), channel_id=1, replica_groups=mesh['src'=8,'tgt'=4] {'src'}, use_global_device_ids=true, to_apply=%region_26.27 | all-reduce | flops 2048 | bytes 16384 | tf_op jit(solution)/shard_map/pmax | solution.py:84
  316.7 14.0 %psum.29 = f32[16,128]{1,0:T(8,128)S(1)} all-reduce(f32[16,128]{1,0:T(8,128)S(1)} %exponential_multiply_fusion.10), channel_id=1, replica_groups=mesh['src'=8,'tgt'=4] {'src'}, use_global_device_ids=true, to_apply=%region_27.28 | all-reduce | flops 2048 | bytes 16384 | tf_op jit(solution)/shard_map/psum | solution.py:85
  330.9 2.4 collective-permute-start.14
  333.3 10.0 %while.100 = (s32[]{:T(128)}, f32[16,128]{1,0:T(8,128)S(1)}, f32[16,128]{1,0:T(8,128)S(1)}, s32[]{:T(128)}, s32[128,2]{0,1:T(2,128)S(1)}, /*index=5*/s32[]{:T(12...) while((s32[]{:T(128)}, f32[16,128]{1,0:T(8,128)S(1)}, ...), condition=%wide.region_33.34_spmd, body=%wide.region_28.33_spmd.sunk | while | flops 34221184 | bytes 2762505 | solution.py:73
  337.6 0.7 scatter_custom_fusion.83
  342.6 0.7 scatter_custom_fusion.83
  343.3 27.3 %pmax.30 = f32[16,128]{1,0:T(8,128)S(1)} all-reduce(f32[16,128]{1,0:T(8,128)S(1)} %max.45), channel_id=1, replica_groups=mesh['src'=8,'tgt'=4] {'tgt'}, use_global_device_ids=true, to_apply=%region_40.41 | all-reduce | flops 2048 | bytes 16384 | tf_op jit(solution)/shard_map/pmax | solution.py:77
  370.7 5.9 %psum.30 = f32[16,128]{1,0:T(8,128)S(1)} all-reduce(f32[16,128]{1,0:T(8,128)S(1)} %exponential_multiply_fusion.9), channel_id=1, replica_groups=mesh['src'=8,'tgt'=4] {'tgt'}, use_global_device_ids=true, to_apply=%region_41.42 | all-reduce | flops 2048 | bytes 16384 | tf_op jit(solution)/shard_map/psum | solution.py:78
  377.2 11.4 %while.102 = (s32[]{:T(128)}, f32[16,128]{1,0:T(8,128)S(1)}, f32[16,128]{1,0:T(8,128)S(1)}, s32[]{:T(128)}, s32[128,2]{0,1:T(2,128)S(1)}, /*index=5*/s32[]{:T(12...) while((s32[]{:T(128)}, f32[16,128]{1,0:T(8,128)S(1)}, ...), condition=%wide.region_47.48_spmd, body=%wide.region_42.47_spmd.sunk | while | flops 34221184 | bytes 2762505 | solution.py:73
  379.8 1.3 gather_fusion.32
  382.2 0.7 scatter_custom_fusion.91
  385.5 1.3 gather_fusion.32
  387.9 0.7 scatter_custom_fusion.91
  388.6 133.4 %pmax.31 = f32[16,128]{1,0:T(8,128)S(1)} all-reduce(f32[16,128]{1,0:T(8,128)S(1)} %get-tuple-element.428), channel_id=1, replica_groups=mesh['src'=8,'tgt'=4] {'src'}, use_global_device_ids=true, to_apply=%region_54.55 | all-reduce | flops 2048 | bytes 16384 | tf_op jit(solution)/shard_map/pmax | solution.py:84
  522.0 14.0 %psum.31 = f32[16,128]{1,0:T(8,128)S(1)} all-reduce(f32[16,128]{1,0:T(8,128)S(1)} %exponential_multiply_fusion.8), channel_id=1, replica_groups=mesh['src'=8,'tgt'=4] {'src'}, use_global_device_ids=true, to_apply=%region_55.56 | all-reduce | flops 2048 | bytes 16384 | tf_op jit(solution)/shard_map/psum | solution.py:85
  (198 shorter events, 35.7 us)
Async XLA Ops:
  1.6 10.5 %copy-start.6 = (bf16[16,128,16]{1,2,0:T(8,128)(2,1)S(1)}, bf16[16,128,16]{1,2,0:T(8,128)(2,1)}, u32[]{:S(2)}) copy-start(bf16[16,128,16]{1,2,0:T(8,128)(2,1)} %param.24) | copy-start | bytes 196612
  9.8 107.6 %collective-permute-start.9 = (bf16[16,128,128]{1,0,2:T(8,128)(2,1)S(1)}, bf16[16,128,128]{1,0,2:T(8,128)(2,1)S(1)}, u32[]{:S(2)}, u32[]{:S(2)}) collective-permute-start(bf16[16,128,128]{1,0,2:T(8,128)(2,1)S(1)} %all_gather.3), channel_id=1, source_target_pairs={{0,16},{16,0},{4,20},{20,4},{8,24},{24,8},{12,28},{28,12},{1,17},{... | collective-permute-start | bytes 1572872 | tf_op jit(solution)/shard_map/ppermute | solution.py:19
  12.4 19.6 %collective-permute-start.1 = (bf16[16,128,16]{2,1,0:T(8,128)(2,1)S(1)}, bf16[16,128,16]{2,1,0:T(8,128)(2,1)S(1)}, u32[]{:S(2)}, u32[]{:S(2)}) collective-permute-start(bf16[16,128,16]{2,1,0:T(8,128)(2,1)S(1)} %copy.18), channel_id=1, source_target_pairs={{0,4},{4,8},{8,12},{12,16},{16,20},{20,24},{24,28},{28,0},{1,5},{5... | collective-permute-start | bytes 196616 | tf_op jit(solution)/shard_map/ppermute | solution.py:111
  16.6 17.9 %collective-permute-start.2 = (bf16[16,128,16]{2,1,0:T(8,128)(2,1)S(1)}, bf16[16,128,16]{2,1,0:T(8,128)(2,1)S(1)}, u32[]{:S(2)}, u32[]{:S(2)}) collective-permute-start(bf16[16,128,16]{2,1,0:T(8,128)(2,1)S(1)} %copy.18), channel_id=1, source_target_pairs={{0,28},{4,0},{8,4},{12,8},{16,12},{20,16},{24,20},{28,24},{1,29},{... | collective-permute-start | bytes 196616 | tf_op jit(solution)/shard_map/ppermute | solution.py:119
  32.0 9.4 %collective-permute-start.3 = (bf16[16,128,16]{2,1,0:T(8,128)(2,1)S(1)}, bf16[16,128,16]{2,1,0:T(8,128)(2,1)S(1)}, u32[]{:S(2)}, u32[]{:S(2)}) collective-permute-start(bf16[16,128,16]{2,1,0:T(8,128)(2,1)S(1)} %collective-permute-done.1), channel_id=1, source_target_pairs={{0,4},{4,8},{8,12},{12,16},{16,20},{20,24},{24,28},{28,0},{1,5},{5... | collective-permute-start | bytes 196616 | tf_op jit(solution)/shard_map/ppermute | solution.py:111
  34.5 35.2 %copy-start.2 = (bf16[16,128,16]{2,1,0:T(8,128)(2,1)}, bf16[16,128,16]{2,1,0:T(8,128)(2,1)S(1)}, u32[]{:S(2)}) copy-start(bf16[16,128,16]{2,1,0:T(8,128)(2,1)S(1)} %collective-permute-done.2) | copy-start | bytes 196612
  34.5 30.6 %collective-permute-start.4 = (bf16[16,128,16]{2,1,0:T(8,128)(2,1)S(1)}, bf16[16,128,16]{2,1,0:T(8,128)(2,1)}, u32[]{:S(2)}, u32[]{:S(2)}) collective-permute-start(bf16[16,128,16]{2,1,0:T(8,128)(2,1)S(1)} %collective-permute-done.2), channel_id=1, source_target_pairs={{0,28},{4,0},{8,4},{12,8},{16,12},{20,16},{24,20},{28,24},{1,29},{... | collective-permute-start | bytes 196616 | tf_op jit(solution)/shard_map/ppermute | solution.py:119
  41.3 28.3 %copy-start.4 = (bf16[16,128,16]{2,1,0:T(8,128)(2,1)}, bf16[16,128,16]{2,1,0:T(8,128)(2,1)S(1)}, u32[]{:S(2)}) copy-start(bf16[16,128,16]{2,1,0:T(8,128)(2,1)S(1)} %collective-permute-done.3) | copy-start | bytes 196612
  41.3 23.8 %collective-permute-start.5 = (bf16[16,128,16]{2,1,0:T(8,128)(2,1)S(1)}, bf16[16,128,16]{2,1,0:T(8,128)(2,1)}, u32[]{:S(2)}, u32[]{:S(2)}) collective-permute-start(bf16[16,128,16]{2,1,0:T(8,128)(2,1)S(1)} %collective-permute-done.3), channel_id=1, source_target_pairs={{0,4},{4,8},{8,12},{12,16},{16,20},{20,24},{24,28},{28,0},{1,5},{5... | collective-permute-start | bytes 196616 | tf_op jit(solution)/shard_map/ppermute | solution.py:111
  65.1 38.8 %collective-permute-start.6 = (bf16[16,128,16]{2,1,0:T(8,128)(2,1)}, bf16[16,128,16]{2,1,0:T(8,128)(2,1)}, u32[]{:S(2)}, u32[]{:S(2)}) collective-permute-start(bf16[16,128,16]{2,1,0:T(8,128)(2,1)} %collective-permute-done.4), channel_id=1, source_target_pairs={{0,28},{4,0},{8,4},{12,8},{16,12},{20,16},{24,20},{28,24},{1,29},{... | collective-permute-start | bytes 196616 | tf_op jit(solution)/shard_map/ppermute | solution.py:119
  65.1 45.5 %collective-permute-start.7 = (bf16[16,128,16]{2,1,0:T(8,128)(2,1)}, bf16[16,128,16]{2,1,0:T(8,128)(2,1)}, u32[]{:S(2)}, u32[]{:S(2)}) collective-permute-start(bf16[16,128,16]{2,1,0:T(8,128)(2,1)} %collective-permute-done.5), channel_id=1, source_target_pairs={{0,4},{4,8},{8,12},{12,16},{16,20},{20,24},{24,28},{28,0},{1,5},{5... | collective-permute-start | bytes 196616 | tf_op jit(solution)/shard_map/ppermute | solution.py:111
  67.9 1.8 copy-start
  67.9 8.8 %collective-permute-start = (s32[]{:T(128)}, s32[]{:T(128)}, u32[]{:S(2)}, u32[]{:S(2)}) collective-permute-start(s32[]{:T(128)} %bitcast.48), channel_id=1, source_target_pairs={{0,16},{16,0},{4,20},{20,4},{8,24},{24,8},{12,28},{28,12},{1,17},{... | collective-permute-start | bytes 20 | tf_op jit(solution)/shard_map/ppermute | solution.py:19
  69.7 48.1 %collective-permute-start.8 = (s32[128,2]{0,1:T(2,128)S(1)}, s32[128,2]{0,1:T(2,128)S(1)}, u32[]{:S(2)}, u32[]{:S(2)}) collective-permute-start(s32[128,2]{0,1:T(2,128)S(1)} %bitcast.228), channel_id=1, source_target_pairs={{0,16},{16,0},{4,20},{20,4},{8,24},{24,8},{12,28},{28,12},{1,17},{... | collective-permute-start | bytes 3080 | tf_op jit(solution)/shard_map/ppermute | solution.py:19
  78.4 2.0 copy-start.3
  80.4 5.1 copy-start.5
  117.8 0.7 copy-start.1
  118.5 13.0 %collective-permute-start.10 = (f32[16,128]{1,0:T(8,128)S(1)}, f32[16,128]{1,0:T(8,128)S(1)}, u32[]{:S(2)}, u32[]{:S(2)}) collective-permute-start(f32[16,128]{1,0:T(8,128)S(1)} %get-tuple-element.415), channel_id=1, source_target_pairs={{0,16},{16,0},{4,20},{20,4},{8,24},{24,8},{12,28},{28,12},{1,17},{... | collective-permute-start | bytes 24584 | tf_op jit(solution)/shard_map/ppermute | solution.py:19
  121.4 47.6 %collective-permute-start.11 = (f32[16,128]{1,0:T(8,128)S(1)}, f32[16,128]{1,0:T(8,128)S(1)}, u32[]{:S(2)}, u32[]{:S(2)}) collective-permute-start(f32[16,128]{1,0:T(8,128)S(1)} %get-tuple-element.417), channel_id=1, source_target_pairs={{0,16},{16,0},{4,20},{20,4},{8,24},{24,8},{12,28},{28,12},{1,17},{... | collective-permute-start | bytes 24584 | tf_op jit(solution)/shard_map/ppermute | solution.py:19
  169.0 5.9 %copy-start.7 = (f32[16,128]{1,0:T(8,128)S(1)}, f32[16,128]{1,0:T(8,128)}, u32[]{:S(2)}) copy-start(f32[16,128]{1,0:T(8,128)} %param.25) | copy-start | bytes 24580
  175.6 17.5 %collective-permute-start.12 = (f32[16,128]{1,0:T(8,128)}, f32[16,128]{1,0:T(8,128)S(1)}, u32[]{:S(2)}, u32[]{:S(2)}) collective-permute-start(f32[16,128]{1,0:T(8,128)} %add_subtract_fusion.3), channel_id=1, source_target_pairs={{0,16},{16,0},{4,20},{20,4},{8,24},{24,8},{12,28},{28,12},{1,17},{... | collective-permute-start | bytes 24584 | tf_op jit(solution)/shard_map/ppermute | solution.py:19
  316.7 14.1 %copy-start.8 = (f32[16,128]{1,0:T(8,128)S(1)}, f32[16,128]{1,0:T(8,128)}, u32[]{:S(2)}) copy-start(f32[16,128]{1,0:T(8,128)} %param.26) | copy-start | bytes 24580
  330.8 12.5 %collective-permute-start.13 = (f32[16,128]{1,0:T(8,128)S(1)}, f32[16,128]{1,0:T(8,128)S(1)}, u32[]{:S(2)}, u32[]{:S(2)}) collective-permute-start(f32[16,128]{1,0:T(8,128)S(1)} %get-tuple-element.423), channel_id=1, source_target_pairs={{0,16},{16,0},{4,20},{20,4},{8,24},{24,8},{12,28},{28,12},{1,17},{... | collective-permute-start | bytes 24584 | tf_op jit(solution)/shard_map/ppermute | solution.py:19
  330.9 39.7 %collective-permute-start.14 = (f32[16,128]{1,0:T(8,128)S(1)}, f32[16,128]{1,0:T(8,128)S(1)}, u32[]{:S(2)}, u32[]{:S(2)}) collective-permute-start(f32[16,128]{1,0:T(8,128)S(1)} %get-tuple-element.425), channel_id=1, source_target_pairs={{0,16},{16,0},{4,20},{20,4},{8,24},{24,8},{12,28},{28,12},{1,17},{... | collective-permute-start | bytes 24584 | tf_op jit(solution)/shard_map/ppermute | solution.py:19
  377.2 11.4 %collective-permute-start.15 = (f32[16,128]{1,0:T(8,128)}, f32[16,128]{1,0:T(8,128)S(1)}, u32[]{:S(2)}, u32[]{:S(2)}) collective-permute-start(f32[16,128]{1,0:T(8,128)} %add_subtract_fusion.1), channel_id=1, source_target_pairs={{0,16},{16,0},{4,20},{20,4},{8,24},{24,8},{12,28},{28,12},{1,17},{... | collective-permute-start | bytes 24584 | tf_op jit(solution)/shard_map/ppermute | solution.py:19
